TPU v7x, 32 devices: a whole 2x2x4 slice. The times are simulated.
32 devices in a mesh: outer: 4 (over y, x), inner: 8 (over z, core).
Axes of the slice: x: 2, y: 2, z: 4, core: 2. Of those that a mesh axis runs over, the one named last changes fastest.
Arguments:
- prim: float32 [8, 384, 512], P(None, ('outer', 'inner')), may hold values from -4 to 9, as said below
- new_owner: int32 [384], replicated, may hold values from 0 to 31, as said below
- new_slot: int32 [384], replicated, may hold values from 0 to 23, as said below
Outputs:
- placed: float32 [8, 768, 512], P(None, ('outer', 'inner'))
Inputs may be any that keep to these rules, and one draw needn't show every extreme that they name: `prim`: field 0 (density) lies in 0.3 to 3 and field 4 (pressure) in 0.2 to 9; fields 1 to 3 are velocities and 5 to 7 the magnetic field. `new_owner`: block g's owner lies in the segment of 8 devices that holds device g // 12 and differs from g // 12 by at most one; owners never fall along g, so every device gets a run of consecutive blocks (possibly none); at most 6 blocks of one device go to each neighbour, and in every draw some device of each segment receives 24 blocks. `new_slot`: the blocks of one owner have slots 0, 1, 2, ... in the order of g.
All inputs are finite; a program needn't handle non-finite values.
Results may differ from a plain program's by a relative error of at most 0.0003.
Values sent between devices are 32-bit elements; how exact they have to be, the bound alone decides.
A program may use at most 64 MiB of HBM per device.

v0:
```python
import jax
import jax.numpy as jnp
from jax import lax
from jax.sharding import PartitionSpec as P

BE = 8
GY = 16


GAMMA = 5.0 / 3.0
COURANT = 0.8


def padded_2(block, sides, width):
    for axis, dim in sides:
        count = lax.axis_size(axis)
        forward = [(i, i + 1) for i in range(count - 1)]
        forward.append((count - 1, 0))
        backward = [(target, source) for source, target in forward]
        low = lax.ppermute(
            lax.slice_in_dim(block, block.shape[dim] - width, None, axis=dim), axis, forward
        )
        high = lax.ppermute(lax.slice_in_dim(block, 0, width, axis=dim), axis, backward)
        block = jnp.concatenate([low, block, high], axis=dim)
    return block


def passed_along(value, axis, steps):
    count = lax.axis_size(axis)
    pairs = [(source, (source + steps) % count) for source in range(count)]
    return lax.ppermute(value, axis, pairs)


def shifted(value, axis, by):
    count = lax.axis_size(axis)
    pairs = [(i, i + by) for i in range(count) if 0 <= i + by < count]
    return lax.ppermute(value, axis, pairs)


def minmod(former, latter):
    return (
        0.5 * (jnp.sign(former) + jnp.sign(latter)) * jnp.minimum(jnp.abs(former), jnp.abs(latter))
    )


def unpack(state):
    return [state[component] for component in range(8)]


def conserved(state):
    density, speed_x, speed_y, speed_z, pressure, field_x, field_y, field_z = unpack(state)
    kinetic = 0.5 * density * (speed_x * speed_x + speed_y * speed_y + speed_z * speed_z)
    magnetic = 0.5 * (field_x * field_x + field_y * field_y + field_z * field_z)
    energy = pressure / (GAMMA - 1.0) + kinetic + magnetic
    return jnp.stack(
        [
            density,
            density * speed_x,
            density * speed_y,
            density * speed_z,
            energy,
            field_x,
            field_y,
            field_z,
        ]
    )


def signal(state):
    density, speed_x, speed_y, speed_z, pressure, field_x, field_y, field_z = unpack(state)
    field_sq = field_x * field_x + field_y * field_y + field_z * field_z
    return (
        jnp.abs(speed_x)
        + jnp.abs(speed_y)
        + jnp.abs(speed_z)
        + 3.0 * jnp.sqrt((GAMMA * pressure + field_sq) / density)
    )


def flux_parts(state, normal):
    density, speed_x, speed_y, speed_z, pressure, field_x, field_y, field_z = unpack(state)
    velocity = (speed_x, speed_y, speed_z)
    magnetic = (field_x, field_y, field_z)
    normal_speed = velocity[normal]
    normal_field = magnetic[normal]
    field_sq = field_x * field_x + field_y * field_y + field_z * field_z
    total_pressure = pressure + 0.5 * field_sq
    conserved_state = conserved(state)
    vel_dot_field = speed_x * field_x + speed_y * field_y + speed_z * field_z
    momentum = []
    for component in range(3):
        momentum_term = (
            density * velocity[component] * normal_speed - magnetic[component] * normal_field
        )
        if component == normal:
            momentum_term = momentum_term + total_pressure
        momentum.append(momentum_term)
    induction = [
        magnetic[component] * normal_speed - velocity[component] * normal_field
        for component in range(3)
    ]
    energy_flux = (
        conserved_state[4] + total_pressure
    ) * normal_speed - normal_field * vel_dot_field
    flux_terms = jnp.stack([density * normal_speed] + momentum + [energy_flux] + induction)
    signal_speed = jnp.abs(normal_speed) + jnp.sqrt((GAMMA * pressure + field_sq) / density)
    return (flux_terms, signal_speed, conserved_state)


def divergence(padded, normal):
    cell_axis = normal + 1
    inner_count = padded.shape[cell_axis] - 4

    def window(values, offset, length):
        return lax.slice_in_dim(values, offset, offset + length, axis=cell_axis)

    steps_between = window(padded, 1, inner_count + 3) - window(padded, 0, inner_count + 3)
    slopes = minmod(
        window(steps_between, 0, inner_count + 2), window(steps_between, 1, inner_count + 2)
    )
    centres = window(padded, 1, inner_count + 2)
    left_state = window(centres, 0, inner_count + 1) + 0.5 * window(slopes, 0, inner_count + 1)
    right_state = window(centres, 1, inner_count + 1) - 0.5 * window(slopes, 1, inner_count + 1)
    flux_left, speed_left, state_left = flux_parts(left_state, normal)
    flux_right, speed_right, state_right = flux_parts(right_state, normal)
    face_flux = 0.5 * (flux_left + flux_right) - 0.5 * jnp.maximum(speed_left, speed_right)[
        None
    ] * (state_right - state_left)
    return window(face_flux, 1, inner_count) - window(face_flux, 0, inner_count)


def advance(x_padded, y_padded, z_padded, time_step):
    middle = x_padded[:, 2:-2]
    change = divergence(x_padded, 0) + divergence(y_padded, 1) + divergence(z_padded, 2)
    return conserved(middle) - time_step * change


def split_blocks(values, blocks):
    leading, first_len, second_len, length = values.shape
    depth = length // blocks
    parted = values.reshape(leading, first_len, second_len, blocks, depth)
    return parted.transpose(0, 3, 1, 2, 4).reshape(leading, blocks, first_len * second_len * depth)


def place(candidates, new_owner, new_slot, device, blocks, reach):
    capacity = blocks + 2 * reach
    block_total = new_owner.shape[0]
    block_ids = device * blocks - reach + jnp.arange(capacity, dtype=jnp.int32)
    inside = (block_ids >= 0) & (block_ids < block_total)
    clipped = jnp.clip(block_ids, 0, block_total - 1)
    owned = inside & (new_owner[clipped] == device)
    slot_ids = jnp.arange(capacity, dtype=jnp.int32)
    chooser = (owned[None, :] & (new_slot[clipped][None, :] == slot_ids[:, None])).astype(
        jnp.float32
    )
    arrived = jnp.einsum("sc,fcx->fsx", chooser, candidates, precision=lax.Precision.HIGHEST)
    return (arrived, jnp.sum(chooser, axis=1))


def per_device(prim, new_owner, new_slot):
    blocks = prim.shape[1]
    edge_len = BE
    length = blocks * edge_len
    reach = blocks // 2
    pencil = (
        prim.reshape(8, blocks, edge_len, edge_len, edge_len)
        .transpose(0, 2, 3, 1, 4)
        .reshape(8, edge_len, edge_len, length)
    )
    fastest = lax.pmax(jnp.max(signal(pencil)), ("outer", "inner"))
    time_step = COURANT / fastest
    device = lax.axis_index(("outer", "inner"))
    y_padded = padded_2(pencil, ((("outer", "inner"), 2),), 2)
    before_x = passed_along(pencil[:, edge_len - 2 :], ("outer", "inner"), GY)
    after_x = passed_along(pencil[:, :2], ("outer", "inner"), -GY)
    x_padded = jnp.concatenate([before_x, pencil, after_x], 1)
    z_padded = jnp.concatenate([pencil[..., -2:], pencil, pencil[..., :2]], 3)
    span = 4 * edge_len

    def advance_group(index):
        offset = index * span
        x_part = lax.dynamic_slice_in_dim(x_padded, offset, span, 3)
        y_part = lax.dynamic_slice_in_dim(y_padded, offset, span, 3)
        z_part = lax.dynamic_slice_in_dim(z_padded, offset, span + 4, 3)
        return advance(x_part, y_part, z_part, time_step)

    result = lax.map(advance_group, jnp.arange(blocks // 4, dtype=jnp.int32))
    result = result.transpose(1, 2, 3, 0, 4).reshape(8, edge_len, edge_len, length)
    updated = split_blocks(result, blocks)
    from_lower = shifted(updated[:, blocks - reach :], "inner", 1)
    from_upper = shifted(updated[:, :reach], "inner", -1)
    candidates = jnp.concatenate([from_lower, updated, from_upper], 1)
    arrived, live = place(candidates, new_owner, new_slot, device, blocks, reach)
    return arrived


def solution(mesh):
    in_specs = (P(None, ("outer", "inner"), None), P(), P())
    out_specs = P(None, ("outer", "inner"), None)
    return jax.shard_map(
        per_device, mesh=mesh, in_specs=in_specs, out_specs=out_specs, check_vma=False
    )
```

profile of v0, /device:TPU:1, one launch (start us, length us, event | category | flops | bytes accessed | tf_op | source)
XLA Modules:
  0.0 105.3 jit_solution(3938059395793438302)
XLA Ops:
  0.0 2.7 %reshape.61 = f32[8,12,8,8,8]{4,3,2,0,1:T(8,128)S(1)} reshape(f32[8,12,512]{2,0,1:T(8,128)} %param.5) | data formatting | bytes 393216 | tf_op jit(solution)/shard_map/reshape | solution.py:166
  2.7 3.8 %copy.5 = f32[8,8,8,12,8]{4,3,2,1,0:T(8,128)} copy(f32[8,8,8,12,8]{4,2,1,0,3:T(8,128)S(1)} %bitcast.35) | data formatting | bytes 393216 | tf_op jit(solution)/shard_map/transpose | solution.py:167
  6.5 3.3 %reshape.62 = f32[8,8,8,96]{3,2,1,0:T(8,128)S(1)} reshape(f32[8,8,8,12,8]{4,3,2,1,0:T(8,128)} %copy.5) | data formatting | bytes 393216 | tf_op jit(solution)/shard_map/reshape | solution.py:168
  9.8 0.7 fusion.40
  10.5 2.7 %collective-permute-start.2 = (f32[8,8,2,96]{3,2,1,0:T(2,128)}, f32[8,8,2,96]{3,2,1,0:T(2,128)S(1)}, u32[]{:S(2)}, u32[]{:S(2)}) collective-permute-start(f32[8,8,2,96]{3,2,1,0:T(2,128)} %get-tuple-element.132), channel_id=1, source_target_pairs={{0,1},{1,2},{2,3},{3,4},{4,5},{5,6},{6,7},{7,8},{8,9},{9,10},{10,1... | collective-permute-start | bytes 147464 | tf_op jit(solution)/shard_map/ppermute | solution.py:20
  13.2 0.7 fusion.41
  13.9 1.2 %collective-permute-start = (f32[8,2,8,96]{3,2,1,0:T(8,128)}, f32[8,2,8,96]{3,2,1,0:T(8,128)}, u32[]{:S(2)}, u32[]{:S(2)}) collective-permute-start(f32[8,2,8,96]{3,2,1,0:T(8,128)} %get-tuple-element.134), channel_id=1, source_target_pairs={{0,16},{1,17},{2,18},{3,19},{4,20},{5,21},{6,22},{7,23},{8,24},{9,... | collective-permute-start | bytes 147464 | tf_op jit(solution)/shard_map/ppermute | solution.py:31
  15.1 0.2 collective-permute-start.1
  15.3 0.9 fusion.39
  16.2 0.9 fusion.30
  17.1 1.2 %pad_maximum_fusion.2 = f32[8,8,8,100]{3,2,1,0:T(8,128)S(1)} fusion(f32[8,8,8,2]{3,2,1,0:T(8,128)} %get-tuple-element.131, f32[8,8,8,96]{3,2,1,0:T(8,128)S(1)} %reshape.62, f32[8,8,8,2]{3,2,1,0:T(8,128)} %get-tuple-element.130), kind=kLoop, calls=%fused_computation.201 | loop fusion | flops 102400 | bytes 409600 | tf_op jit(solution)/shard_map/concatenate | solution.py:177
  18.4 40.7 %pmax.7 = f32[]{:T(128)} all-reduce(f32[]{:T(128)} %fusion.30), channel_id=1, replica_groups=mesh['outer'=4,'inner'=8] {'outer','inner'}, use_global_device_ids=true, to_apply=%region_1.0 | all-reduce | flops 1 | bytes 8 | tf_op jit(solution)/shard_map/pmax | solution.py:170
  59.6 0.7 gather_fusion
  60.5 0.9 pad_maximum_fusion.1
  61.4 21.1 %while.10 = (s32[]{:T(128)}, f32[3,8,8,8,32]{4,3,2,1,0:T(8,128)}, s32[3]{0:T(128)S(1)}, f32[8,12,8,96]{3,2,1,0:T(8,128)S(1)}, f32[]{:T(128)}, /*index=5*/f32[8,8...) while((s32[]{:T(128)}, f32[3,8,8,8,32]{4,3,2,1,0:T(8,128)}, ...), condition=%wide.region_3.4_spmd, body=%wide.region_2.3_spmd.sunk | while | flops 1960325 | bytes 22909688 | solution.py:187
  61.4 0.6 dynamic_slice.14
  62.6 0.3 dynamic-slice_subtract_fusion.8
  63.0 0.2 fusion.48
  63.8 0.3 dynamic-slice_subtract_fusion.7
  64.1 0.4 minimum_multiply_fusion.7
  64.5 0.4 fusion.47
  66.2 0.3 fusion.46
  67.6 0.8 fusion.49
  68.5 0.6 dynamic_slice.14
  69.6 0.3 dynamic-slice_subtract_fusion.8
  70.0 0.2 fusion.48
  70.8 0.3 dynamic-slice_subtract_fusion.7
  71.1 0.4 minimum_multiply_fusion.7
  71.5 0.4 fusion.47
  73.2 0.3 fusion.46
  74.6 0.8 fusion.49
  75.5 0.6 dynamic_slice.14
  76.7 0.3 dynamic-slice_subtract_fusion.8
  77.1 0.2 fusion.48
  77.8 0.3 dynamic-slice_subtract_fusion.7
  78.2 0.4 minimum_multiply_fusion.7
  78.5 0.4 fusion.47
  80.2 0.3 fusion.46
  81.7 0.9 fusion.49
  82.5 1.7 %copy.6 = f32[8,8,8,3,32]{4,3,2,1,0:T(4,128)S(1)} copy(f32[8,8,8,3,32]{4,2,1,0,3:T(8,128)} %bitcast.38) | data formatting | bytes 393216 | tf_op jit(solution)/shard_map/transpose | solution.py:188
  84.2 2.8 %reshape_reshape.3 = f32[8,8,8,12,8]{4,3,2,1,0:T(8,128)} reshape(f32[8,8,8,3,32]{4,3,2,1,0:T(4,128)S(1)} %copy.6) | data formatting | bytes 393216 | tf_op jit(solution)/shard_map/reshape;reshape | solution.py:141
  87.0 3.1 %copy.11 = f32[8,12,8,8,8]{4,3,2,1,0:T(8,128)S(1)} copy(f32[8,12,8,8,8]{4,1,3,2,0:T(8,128)} %bitcast.37) | data formatting | bytes 393216 | tf_op jit(solution)/shard_map/reshape | solution.py:142
  90.1 2.0 %reshape.81 = f32[8,12,512]{2,1,0:T(8,128)S(1)} reshape(f32[8,12,8,8,8]{4,3,2,1,0:T(8,128)S(1)} %copy.11) | data formatting | bytes 393216 | tf_op jit(solution)/shard_map/reshape | solution.py:142
  92.1 5.7 %collective-permute-start.4 = (f32[8,6,512]{2,1,0:T(8,128)S(1)}, f32[8,6,512]{2,1,0:T(8,128)S(1)}, u32[]{:S(2)}, u32[]{:S(2)}) collective-permute-start(f32[8,6,512]{2,1,0:T(8,128)S(1)} %get-tuple-element.128), channel_id=1, source_target_pairs={{0,1},{1,2},{2,3},{3,4},{4,5},{5,6},{6,7},{8,9},{9,10},{10,11},{11... | collective-permute-start | bytes 294920 | tf_op jit(solution)/shard_map/ppermute | solution.py:37
  97.9 1.9 %collective-permute-start.5 = (f32[8,6,512]{2,1,0:T(8,128)S(1)}, f32[8,6,512]{2,1,0:T(8,128)S(1)}, u32[]{:S(2)}, u32[]{:S(2)}) collective-permute-start(f32[8,6,512]{2,1,0:T(8,128)S(1)} %get-tuple-element.129), channel_id=1, source_target_pairs={{1,0},{2,1},{3,2},{4,3},{5,4},{6,5},{7,6},{9,8},{10,9},{11,10},{12... | collective-permute-start | bytes 294920 | tf_op jit(solution)/shard_map/ppermute | solution.py:37
  99.8 0.7 gather_fusion.1
  100.5 3.6 %collective-permute-done.5 = f32[8,6,512]{2,1,0:T(8,128)S(1)} collective-permute-done((f32[8,6,512]{2,1,0:T(8,128)S(1)}, f32[8,6,512]{2,1,0:T(8,128)S(1)}, u32[]{:S(2)}, u32[]{:S(2)}) %collective-permute-start.5) | collective-permute-done | bytes 98336 | tf_op jit(solution)/shard_map/ppermute | solution.py:37
  104.1 1.1 %convolution_bitcast_fusion = f32[8,24,512]{2,1,0:T(8,128)} fusion(f32[8,6,512]{2,1,0:T(8,128)S(1)} %collective-permute-done.5, f32[8,12,512]{2,1,0:T(8,128)S(1)} %reshape.81, f32[8,6,512]{2,1,0:T(8,128)S(1)} %collective-permute-done.4, s32[24]{0:T(128)S(1)} %gather_fusion.1, pred[24]{0:T(512)(128)(4,1)S(1)} %compare_and_fusion), kind=kOutput, calls=%fused_computation.176 | convolution fusion | flops 28509312 | bytes 786552 | tf_op jit(solution)/shard_map/sc,fcx->fsx/dot_general | solution.py:156
  (239 shorter events, 8.0 us)
Async XLA Ops:
  0.0 59.6 %copy-start = (s32[384]{0:T(512)S(1)}, s32[384]{0:T(512)}, u32[]{:S(2)}) copy-start(s32[384]{0:T(512)} %param.6) | copy-start | bytes 4612
  10.5 49.8 %collective-permute-start.2 = (f32[8,8,2,96]{3,2,1,0:T(2,128)}, f32[8,8,2,96]{3,2,1,0:T(2,128)S(1)}, u32[]{:S(2)}, u32[]{:S(2)}) collective-permute-start(f32[8,8,2,96]{3,2,1,0:T(2,128)} %get-tuple-element.132), channel_id=1, source_target_pairs={{0,1},{1,2},{2,3},{3,4},{4,5},{5,6},{6,7},{7,8},{8,9},{9,10},{10,1... | collective-permute-start | bytes 147464 | tf_op jit(solution)/shard_map/ppermute | solution.py:20
  13.2 47.2 %collective-permute-start.3 = (f32[8,8,2,96]{3,2,1,0:T(2,128)}, f32[8,8,2,96]{3,2,1,0:T(2,128)S(1)}, u32[]{:S(2)}, u32[]{:S(2)}) collective-permute-start(f32[8,8,2,96]{3,2,1,0:T(2,128)} %get-tuple-element.133), channel_id=1, source_target_pairs={{1,0},{2,1},{3,2},{4,3},{5,4},{6,5},{7,6},{8,7},{9,8},{10,9},{11,1... | collective-permute-start | bytes 147464 | tf_op jit(solution)/shard_map/ppermute | solution.py:23
  13.9 46.6 %collective-permute-start = (f32[8,2,8,96]{3,2,1,0:T(8,128)}, f32[8,2,8,96]{3,2,1,0:T(8,128)}, u32[]{:S(2)}, u32[]{:S(2)}) collective-permute-start(f32[8,2,8,96]{3,2,1,0:T(8,128)} %get-tuple-element.134), channel_id=1, source_target_pairs={{0,16},{1,17},{2,18},{3,19},{4,20},{5,21},{6,22},{7,23},{8,24},{9,... | collective-permute-start | bytes 147464 | tf_op jit(solution)/shard_map/ppermute | solution.py:31
  15.1 45.4 %collective-permute-start.1 = (f32[8,2,8,96]{3,2,1,0:T(8,128)}, f32[8,2,8,96]{3,2,1,0:T(8,128)}, u32[]{:S(2)}, u32[]{:S(2)}) collective-permute-start(f32[8,2,8,96]{3,2,1,0:T(8,128)} %get-tuple-element.135), channel_id=1, source_target_pairs={{0,16},{1,17},{2,18},{3,19},{4,20},{5,21},{6,22},{7,23},{8,24},{9,... | collective-permute-start | bytes 147464 | tf_op jit(solution)/shard_map/ppermute | solution.py:31
  90.1 9.7 %copy-start.1 = (s32[384]{0:T(512)S(1)}, s32[384]{0:T(512)}, u32[]{:S(2)}) copy-start(s32[384]{0:T(512)} %param.7) | copy-start | bytes 4612
  92.1 8.4 %collective-permute-start.4 = (f32[8,6,512]{2,1,0:T(8,128)S(1)}, f32[8,6,512]{2,1,0:T(8,128)S(1)}, u32[]{:S(2)}, u32[]{:S(2)}) collective-permute-start(f32[8,6,512]{2,1,0:T(8,128)S(1)} %get-tuple-element.128), channel_id=1, source_target_pairs={{0,1},{1,2},{2,3},{3,4},{4,5},{5,6},{6,7},{8,9},{9,10},{10,11},{11... | collective-permute-start | bytes 294920 | tf_op jit(solution)/shard_map/ppermute | solution.py:37
  97.9 6.3 %collective-permute-start.5 = (f32[8,6,512]{2,1,0:T(8,128)S(1)}, f32[8,6,512]{2,1,0:T(8,128)S(1)}, u32[]{:S(2)}, u32[]{:S(2)}) collective-permute-start(f32[8,6,512]{2,1,0:T(8,128)S(1)} %get-tuple-element.129), channel_id=1, source_target_pairs={{1,0},{2,1},{3,2},{4,3},{5,4},{6,5},{7,6},{9,8},{10,9},{11,10},{12... | collective-permute-start | bytes 294920 | tf_op jit(solution)/shard_map/ppermute | solution.py:37
where the time goes:
time: 106 us; the launch traced here: 105 us
  blocking collectives  40.7 us (38%)
  local copies, waits for them, and re-layouts  25.7 us (24%)
  other arithmetic  18.2 us (17%)
  starting transfers between devices  11.8 us (11%)
  waiting for transfers between devices  3.63 us (3%)
  loops' own time  3.46 us (3%)
  matrix products  1.11 us (1%)
    pmax x1, blocking collectives, per_device(): fastest = lax.pmax(jnp.max(signal(pencil)), ('outer', 'inner'))  40.7 us
    ppermute x2, starting transfers between devices, shifted(): return lax.ppermute(value, axis, pairs)  7.62 us
    reshape x2, local copies, waits for them, and re-layouts, split_blocks(): parted.transpose(0, 3, 1, 2, 4)  5.12 us
    transpose x1, local copies, waits for them, and re-layouts, per_device(): pencil = prim.reshape(8, blocks, edge_len, edge_len, edge_len).transpose(...  3.81 us
    ppermute x2, waiting for transfers between devices, shifted(): return lax.ppermute(value, axis, pairs)  3.62 us
    while x144, other arithmetic  3.57 us
    another operation x1, loops' own time, per_device(): result = lax.map(advance_group, jnp.arange(blocks // 4, dtype=jnp.int32))  3.46 us
    reshape x1, local copies, waits for them, and re-layouts, per_device(): pencil = prim.reshape(8, blocks, edge_len, edge_len, edge_len).transpose(...  3.32 us
  transfers between devices with their start and end apart: 6, of which 1 were waited for; matrix products, arithmetic and copies ran while one was open for 5% of the time, Pallas kernels for 0%

commit v1 on v0

v1 whole, which is shorter than its diff:
```python
import functools

import jax
import jax.numpy as jnp
from jax import lax
from jax.experimental import pallas as pl
from jax.experimental.pallas import tpu as pltpu
from jax.sharding import PartitionSpec as P

BE = 8
GY = 16
LANES = 128

GAMMA = 5.0 / 3.0
COURANT = 0.8
MESH = pl.DeviceIdType.MESH


def turn(value, by):
    return pltpu.roll(value, by % LANES, 1)


def half_slope(former, latter):
    low = jnp.minimum(former, latter)
    high = jnp.maximum(former, latter)
    return 0.5 * (jnp.maximum(low, 0.0) + jnp.minimum(high, 0.0))


def sound(density, pressure, field_sq):
    total = GAMMA * pressure + field_sq
    return total * lax.rsqrt(total * density)


def flux_parts(state, normal):
    density, pressure = state[0], state[4]
    vel = state[1:4]
    mag = state[5:8]
    vn, bn = vel[normal], mag[normal]
    field_sq = mag[0] * mag[0] + mag[1] * mag[1] + mag[2] * mag[2]
    speed_sq = vel[0] * vel[0] + vel[1] * vel[1] + vel[2] * vel[2]
    half_field = 0.5 * field_sq
    energy = pressure * (1.0 / (GAMMA - 1.0)) + 0.5 * density * speed_sq + half_field
    total_pressure = pressure + half_field
    vel_dot = vel[0] * mag[0] + vel[1] * mag[1] + vel[2] * mag[2]
    mom = [density * v for v in vel]
    flux_mom = []
    for k in range(3):
        term = mom[k] * vn - mag[k] * bn
        if k == normal:
            term = term + total_pressure
        flux_mom.append(term)
    induction = [None if k == normal else mag[k] * vn - vel[k] * bn for k in range(3)]
    flux = [mom[normal]] + flux_mom + [(energy + total_pressure) * vn - bn * vel_dot] + induction
    speed = jnp.abs(vn) + sound(density, pressure, field_sq)
    return flux, speed, [density] + mom + [energy] + list(mag)


def face_flux(left, right, normal):
    flux_l, speed_l, cons_l = flux_parts(left, normal)
    flux_r, speed_r, cons_r = flux_parts(right, normal)
    half = 0.5 * jnp.maximum(speed_l, speed_r)
    out = []
    for k in range(8):
        upwind = half * (cons_r[k] - cons_l[k])
        if flux_l[k] is None:
            out.append(-upwind)
        else:
            out.append(0.5 * (flux_l[k] + flux_r[k]) - upwind)
    return out


def conserved(state):
    density, pressure = state[0], state[4]
    vel, mag = state[1:4], state[5:8]
    kinetic = 0.5 * density * (vel[0] * vel[0] + vel[1] * vel[1] + vel[2] * vel[2])
    magnetic = 0.5 * (mag[0] * mag[0] + mag[1] * mag[1] + mag[2] * mag[2])
    energy = pressure * (1.0 / (GAMMA - 1.0)) + kinetic + magnetic
    return [density] + [density * v for v in vel] + [energy] + list(mag)


def step_kernel(
    count_o, count_i, blocks, reach,
    prim, own, lower, upper,
    wrap, change, x_before, x_after, y_send, y_before, y_after,
    top_send, top_in, top_send2, top_in2, move_low, move_high,
    x_sem, y_sem, in_sem, out_sem, low_sem, high_sem,
):
    tiles = prim.shape[2] // LANES
    total = count_o * count_i
    o, i = lax.axis_index("outer"), lax.axis_index("inner")
    me = o * count_i + i

    def place_of(step):
        flat = lax.rem(me + (step % total), total)
        return (lax.div(flat, count_i), lax.rem(flat, count_i))

    inner_ids = [(o, lax.rem(i + k, count_i)) for k in range(1, count_i)]
    outer_ids = [(lax.rem(o + k, count_o), i) for k in range(1, count_o)]
    greeted = inner_ids + outer_ids + [place_of(s) for s in (1, -1, GY, -GY)]
    barrier = pltpu.get_barrier_semaphore()
    for target in greeted:
        pl.semaphore_signal(barrier, inc=1, device_id=target, device_id_type=MESH)

    def send(src, dst, sems, index, target):
        copy = pltpu.make_async_remote_copy(
            src_ref=src, dst_ref=dst, send_sem=sems.at[0, index], recv_sem=sems.at[1, index],
            device_id=target, device_id_type=MESH,
        )
        return copy

    def lanes(t):
        return pl.ds(t * LANES, LANES)

    def load(t):
        return [prim[f, :, lanes(t)] for f in range(8)]

    lane = lax.broadcasted_iota(jnp.int32, (blocks, LANES), 1)
    quarter = lax.rem(lane, 64) // 16
    first_half = lane < 64
    even = lax.rem(lane, 16) < 8
    y_of = lax.rem(lane, 64) // 8
    z_of = lax.rem(lane, 8)
    y_first, y_last = y_of == 0, y_of == BE - 1
    z_first, z_last = z_of == 0, z_of == BE - 1

    top = None
    for t in range(tiles):
        w = load(t)
        field_sq = w[5] * w[5] + w[6] * w[6] + w[7] * w[7]
        signal = jnp.abs(w[1]) + jnp.abs(w[2]) + jnp.abs(w[3]) + 3.0 * sound(w[0], w[4], field_sq)
        top = signal if top is None else jnp.maximum(top, signal)
    top_send[...] = jnp.max(top, axis=0, keepdims=True)

    for f in range(8):
        low = high = None
        for t in range(tiles):
            w = prim[f, :, lanes(t)]
            a, b = turn(w, 16 * t), turn(w, 16 * t - 48)
            low = a if low is None else jnp.where(quarter == t, a, low)
            high = b if high is None else jnp.where(quarter == t, b, high)
        y_send[0, f] = low
        y_send[1, f] = high
    for f in range(8):
        wrap[f, pl.ds(1, blocks), :] = prim[f]
        wrap[f, pl.ds(0, 1), :] = prim[f, pl.ds(blocks - 1, 1), :]
        wrap[f, pl.ds(blocks + 1, 1), :] = prim[f, pl.ds(0, 1), :]

    pl.semaphore_wait(barrier, len(greeted))

    last = lanes(tiles - 1)
    x_copies = [
        send(prim.at[:, :, last], x_before, x_sem, 0, place_of(GY)),
        send(prim.at[:, :, lanes(0)], x_after, x_sem, 1, place_of(-GY)),
    ]
    y_copies = [
        send(y_send.at[1], y_before, y_sem, 0, place_of(1)),
        send(y_send.at[0], y_after, y_sem, 1, place_of(-1)),
    ]
    in_copies = [
        send(top_send, top_in.at[k], in_sem, k, inner_ids[k]) for k in range(count_i - 1)
    ]
    for copy in y_copies + in_copies + x_copies:
        copy.start()

    def next_row(v):
        return jnp.concatenate([v[1:], v[:1]], axis=0)

    def prev_row(v):
        return jnp.concatenate([v[blocks - 1 :], v[: blocks - 1]], axis=0)

    for t in range(tiles):
        w = load(t)
        left, right = [], []
        for f in range(8):
            up = jnp.where(z_last, turn(wrap[f, pl.ds(2, blocks), lanes(t)], 7), turn(w[f], -1))
            down = jnp.where(z_first, turn(wrap[f, pl.ds(0, blocks), lanes(t)], -7), turn(w[f], 1))
            h = half_slope(w[f] - down, up - w[f])
            r = w[f] - h
            left.append(w[f] + h)
            right.append(jnp.where(z_last, turn(next_row(r), 7), turn(r, -1)))
        g = face_flux(left, right, 2)
        for f in range(8):
            before = jnp.where(z_first, turn(prev_row(g[f]), -7), turn(g[f], 1))
            change[f, :, lanes(t)] = g[f] - before

    for copy in in_copies:
        copy.wait()
    row = top_send[...]
    for k in range(count_i - 1):
        row = jnp.maximum(row, top_in[k])
    top_send2[...] = row
    out_copies = [
        send(top_send2, top_in2.at[k], out_sem, k, outer_ids[k]) for k in range(count_o - 1)
    ]
    for copy in out_copies:
        copy.start()

    for copy in x_copies:
        copy.wait()

    def cells_x(t):
        if t < 0:
            return [x_before[f] for f in range(8)]
        if t >= tiles:
            return [x_after[f] for f in range(8)]
        return load(t)

    def shift_x(low_tile, high_tile):
        return turn(jnp.where(first_half, low_tile, high_tile), 64)

    here = cells_x(-1)
    dp_prev = g_prev = None
    held = None
    for t in range(-1, tiles + 1):
        after = cells_x(t + 1) if t < tiles else here
        left, right, dps = [], [], []
        for f in range(8):
            dp = shift_x(after[f], here[f]) - here[f]
            dm = shift_x(dp, dp if dp_prev is None else dp_prev[f])
            h = half_slope(dm, dp)
            dps.append(dp)
            left.append(here[f] + h)
            right.append(here[f] - h)
        if held is not None:
            old_left, old_right = held
            g = face_flux(old_left, [shift_x(right[f], old_right[f]) for f in range(8)], 0)
            if g_prev is not None:
                for f in range(8):
                    spot = (f, slice(None), lanes(t - 1))
                    change[spot] = change[spot] + (g[f] - shift_x(g[f], g_prev[f]))
            g_prev = g
        held = (left, right)
        dp_prev = dps
        here = after

    for copy in y_copies:
        copy.wait()
    ghosts = []
    left, right = [], []
    for f in range(8):
        low_own, high_own = y_send[0, f], y_send[1, f]
        before, after = y_before[f], y_after[f]
        a = jnp.where(even, high_own, turn(before, 72))
        b = jnp.where(even, turn(high_own, -8), turn(before, 64))
        c = jnp.where(even, after, turn(low_own, 72))
        d = jnp.where(even, turn(after, -8), turn(low_own, 64))
        mid = c - b
        left.append(b + half_slope(b - a, mid))
        right.append(c - half_slope(mid, d - c))
        ghosts.append(jnp.where(even, c, b))
    edge = face_flux(left, right, 1)

    for copy in out_copies:
        copy.wait()
    row = top_send2[...]
    for k in range(count_o - 1):
        row = jnp.maximum(row, top_in2[k])
    time_step = COURANT / jnp.max(row, axis=1, keepdims=True)

    to_low = [
        send(move_low.at[:, :, lanes(t)], upper.at[:, :, lanes(t)], low_sem, t, (o, lax.rem(i + count_i - 1, count_i)))
        for t in range(tiles)
    ]
    to_high = [
        send(move_high.at[:, :, lanes(t)], lower.at[:, :, lanes(t)], high_sem, t, (o, lax.rem(i + 1, count_i)))
        for t in range(tiles)
    ]
    for t in range(tiles):
        w = load(t)
        back = 56 - 16 * t
        left, right = [], []
        for f in range(8):
            ghost = turn(ghosts[f], back)
            up = jnp.where(y_last, ghost, turn(w[f], -8))
            down = jnp.where(y_first, ghost, turn(w[f], 8))
            h = half_slope(w[f] - down, up - w[f])
            left.append(w[f] + h)
            right.append(turn(w[f] - h, -8))
        g = face_flux(left, right, 1)
        cons = conserved(w)
        for f in range(8):
            rim = turn(edge[f], back)
            face = jnp.where(y_last, rim, g[f])
            before = jnp.where(y_first, rim, turn(g[f], 8))
            result = cons[f] - time_step * (change[f, :, lanes(t)] + (face - before))
            own[f, :, lanes(t)] = result
            move_low[f, :, lanes(t)] = result[:reach]
            move_high[f, :, lanes(t)] = result[blocks - reach :]

        @pl.when(i > 0)
        def _():
            to_low[t].start()

        @pl.when(i < count_i - 1)
        def _():
            to_high[t].start()

    @pl.when(i > 0)
    def _():
        for t in range(tiles):
            to_low[t].wait_send()
            to_high[t].wait_recv()

    @pl.when(i < count_i - 1)
    def _():
        for t in range(tiles):
            to_high[t].wait_send()
            to_low[t].wait_recv()


def place_kernel(blocks, reach, block_total, count_i, owner, own, lower, upper, out, wide):
    me = lax.axis_index("outer") * count_i + lax.axis_index("inner")
    capacity = blocks + 2 * reach
    start = jnp.int32(capacity)
    count = jnp.int32(0)
    for c in range(capacity):
        g = me * blocks - reach + c
        inside = (g >= 0) & (g < block_total)
        mine = inside & (owner[jnp.clip(g, 0, block_total - 1)] == me)
        count = count + mine.astype(jnp.int32)
        start = jnp.where(mine, jnp.minimum(start, c), start)
    start = jnp.where(count > 0, start, 0)
    row = lax.broadcasted_iota(jnp.int32, (capacity, own.shape[2]), 0)
    live = row < count
    for f in range(8):
        wide[f, pl.ds(0, reach), :] = lower[f]
        wide[f, pl.ds(reach, blocks), :] = own[f]
        wide[f, pl.ds(reach + blocks, reach), :] = upper[f]
    for f in range(8):
        out[f] = jnp.where(live, pltpu.roll(wide[f], capacity - start, 0), 0.0)


def per_device(count_o, count_i, prim, new_owner, new_slot):
    blocks, cells = prim.shape[1:]
    reach = blocks // 2
    tiles = cells // LANES
    vmem = pl.BlockSpec(memory_space=pltpu.VMEM)
    f32 = jnp.float32
    dma = pltpu.SemaphoreType.DMA
    own, lower, upper = pl.pallas_call(
        functools.partial(step_kernel, count_o, count_i, blocks, reach),
        out_shape=[
            jax.ShapeDtypeStruct((8, blocks, cells), f32),
            jax.ShapeDtypeStruct((8, reach, cells), f32),
            jax.ShapeDtypeStruct((8, reach, cells), f32),
        ],
        in_specs=[vmem],
        out_specs=[vmem] * 3,
        scratch_shapes=[
            pltpu.VMEM((8, blocks + 4, cells), f32),
            pltpu.VMEM((8, blocks, cells), f32),
            pltpu.VMEM((8, blocks, LANES), f32),
            pltpu.VMEM((8, blocks, LANES), f32),
            pltpu.VMEM((2, 8, blocks, LANES), f32),
            pltpu.VMEM((8, blocks, LANES), f32),
            pltpu.VMEM((8, blocks, LANES), f32),
            pltpu.VMEM((1, LANES), f32),
            pltpu.VMEM((count_i - 1, 1, LANES), f32),
            pltpu.VMEM((1, LANES), f32),
            pltpu.VMEM((count_o - 1, 1, LANES), f32),
            pltpu.VMEM((8, reach, cells), f32),
            pltpu.VMEM((8, reach, cells), f32),
            dma((2, 2)),
            dma((2, 2)),
            dma((2, count_i - 1)),
            dma((2, count_o - 1)),
            dma((2, tiles)),
            dma((2, tiles)),
        ],
        compiler_params=pltpu.CompilerParams(collective_id=0, has_side_effects=True),
        name="step",
    )(prim)
    capacity = blocks + 2 * reach
    return pl.pallas_call(
        functools.partial(place_kernel, blocks, reach, new_owner.shape[0], count_i),
        out_shape=jax.ShapeDtypeStruct((8, capacity, cells), f32),
        in_specs=[pl.BlockSpec(memory_space=pltpu.SMEM), vmem, vmem, vmem],
        out_specs=vmem,
        scratch_shapes=[pltpu.VMEM((8, capacity, cells), f32)],
        name="place",
    )(new_owner, own, lower, upper)


def solution(mesh):
    in_specs = (P(None, ("outer", "inner"), None), P(), P())
    out_specs = P(None, ("outer", "inner"), None)
    run = functools.partial(per_device, mesh.shape["outer"], mesh.shape["inner"])
    return jax.shard_map(
        run, mesh=mesh, in_specs=in_specs, out_specs=out_specs, check_vma=False
    )
```

time: 106 us -> 21.8 us (0.21)
  blocking collectives: 40.7 us -> 0 us
  local copies, waits for them, and re-layouts: 25.7 us -> 1.75 us
  Pallas kernels: 0 us -> 19.9 us
  other arithmetic: 18.2 us -> 0 us
  starting transfers between devices: 11.8 us -> 0 us
  waiting for transfers between devices: 3.63 us -> 0 us
  loops' own time: 3.46 us -> 0 us
  matrix products: 1.11 us -> 0 us
    pmax x1 -> x0, blocking collectives: 40.7 us -> none  [per_device(): fastest = lax.pmax(jnp.max(signal(pencil)), ('outer', 'inner'))]
    pallas_call x0 -> x2, Pallas kernels: none -> 19.9 us  [the longest x1 17.9 us: per_device(): pl.pallas_call(functools.partial(step_kernel, count_o, count_i, blocks, r...]
    ppermute x6 -> x0, starting transfers between devices: 11.8 us -> none  [the longest x2 7.62 us: shifted(): return lax.ppermute(value, axis, pairs)]
    reshape x4 -> x0, local copies, waits for them, and re-layouts: 11.1 us -> none  [the longest x2 5.12 us: split_blocks(): parted.transpose(0, 3, 1, 2, 4)]
    transpose x2 -> x0, local copies, waits for them, and re-layouts: 5.48 us -> none  [the longest x1 3.81 us: per_device(): pencil = prim.reshape(8, blocks, edge_len, edge_len, edge_len).transpose(...]
    ppermute x6 -> x0, waiting for transfers between devices: 3.63 us -> none  [the longest x2 3.62 us: shifted(): return lax.ppermute(value, axis, pairs)]
    while x144 -> x0, other arithmetic: 3.57 us -> none
    another operation x1 -> x0, loops' own time: 3.46 us -> none  [per_device(): result = lax.map(advance_group, jnp.arange(blocks // 4, dtype=jnp.int32))]
  transfers between devices with their start and end apart: 6 -> 0, of which waited for: 1 -> 0; matrix products, arithmetic and copies ran while one was open for 5% -> 0% of each run, Pallas kernels for 0% -> 0%
where the time goes in v1:
time: 21.8 us; the launch traced here: 21.6 us
  Pallas kernels  19.9 us (91%)
  local copies, waits for them, and re-layouts  1.75 us (8%)
    pallas_call x1, Pallas kernels, per_device(): pl.pallas_call(functools.partial(step_kernel, count_o, count_i, blocks, r...  17.9 us
    pallas_call x1, Pallas kernels, per_device(): pl.pallas_call(functools.partial(place_kernel, blocks, reach, new_owner.s...  2 us
    unnamed x1, local copies, waits for them, and re-layouts  1.75 us

profile of v1, /device:TPU:1, one launch (start us, length us, event | category | flops | bytes accessed | tf_op | source)
XLA Modules:
  0.0 21.6 jit_solution(11307000563616609720)
XLA Ops:
  0.0 1.7 %copy.3.prim = f32[8,12,512]{2,1,0:T(8,128)} copy(f32[8,12,512]{2,0,1:T(8,128)} %param.3) | data formatting | bytes 393216 | tf_op args[0]
  1.7 17.9 %step.1 = (f32[8,12,512]{2,1,0:T(8,128)}, f32[8,6,512]{2,1,0:T(8,128)}, f32[8,6,512]{2,1,0:T(8,128)}) custom-call(f32[8,12,512]{2,1,0:T(8,128)} %copy.3.prim), custom_call_target="tpu_custom_call" | custom-call | tf_op jit(solution)/shard_map/step/pallas_call | solution.py:340
  19.6 2.0 %place.1 = f32[8,24,512]{2,1,0:T(8,128)} custom-call(s32[384]{0:T(512)} %owner.1, f32[8,12,512]{2,1,0:T(8,128)} %get-tuple-element.8.own, f32[8,6,512]{2,1,0:T(8,128)} %get-tuple-element.9.lower, f32[8,6,512]{2,1,0:T(8,128)} %get-tuple-element.10.upper), custom_call_target="tpu_custom_call" | custom-call | tf_op jit(solution)/shard_map/place/pallas_call | solution.py:374

commit v2 on v1

v2 whole, which is shorter than its diff:
```python
import functools

import jax
import jax.numpy as jnp
from jax import lax
from jax.experimental import pallas as pl
from jax.experimental.pallas import tpu as pltpu
from jax.sharding import PartitionSpec as P

BE = 8
GY = 16
LANES = 128

GAMMA = 5.0 / 3.0
COURANT = 0.8
MESH = pl.DeviceIdType.MESH


def turn(value, by):
    return pltpu.roll(value, by % LANES if isinstance(by, int) else by, 1)


def half_slope(former, latter):
    low = jnp.minimum(former, latter)
    high = jnp.maximum(former, latter)
    return 0.5 * (jnp.maximum(low, 0.0) + jnp.minimum(high, 0.0))


def sound(density, pressure, field_sq):
    total = GAMMA * pressure + field_sq
    return total * lax.rsqrt(total * density)


def flux_parts(state, normal):
    density, pressure = state[0], state[4]
    vel = state[1:4]
    mag = state[5:8]
    vn, bn = vel[normal], mag[normal]
    field_sq = mag[0] * mag[0] + mag[1] * mag[1] + mag[2] * mag[2]
    speed_sq = vel[0] * vel[0] + vel[1] * vel[1] + vel[2] * vel[2]
    half_field = 0.5 * field_sq
    energy = pressure * (1.0 / (GAMMA - 1.0)) + 0.5 * density * speed_sq + half_field
    total_pressure = pressure + half_field
    vel_dot = vel[0] * mag[0] + vel[1] * mag[1] + vel[2] * mag[2]
    mom = [density * v for v in vel]
    flux_mom = []
    for k in range(3):
        term = mom[k] * vn - mag[k] * bn
        if k == normal:
            term = term + total_pressure
        flux_mom.append(term)
    induction = [None if k == normal else mag[k] * vn - vel[k] * bn for k in range(3)]
    flux = [mom[normal]] + flux_mom + [(energy + total_pressure) * vn - bn * vel_dot] + induction
    speed = jnp.abs(vn) + sound(density, pressure, field_sq)
    return flux, speed, [density] + mom + [energy] + list(mag)


def face_flux(left, right, normal):
    flux_l, speed_l, cons_l = flux_parts(left, normal)
    flux_r, speed_r, cons_r = flux_parts(right, normal)
    half = 0.5 * jnp.maximum(speed_l, speed_r)
    out = []
    for k in range(8):
        upwind = half * (cons_r[k] - cons_l[k])
        if flux_l[k] is None:
            out.append(-upwind)
        else:
            out.append(0.5 * (flux_l[k] + flux_r[k]) - upwind)
    return out


def conserved(state):
    density, pressure = state[0], state[4]
    vel, mag = state[1:4], state[5:8]
    kinetic = 0.5 * density * (vel[0] * vel[0] + vel[1] * vel[1] + vel[2] * vel[2])
    magnetic = 0.5 * (mag[0] * mag[0] + mag[1] * mag[1] + mag[2] * mag[2])
    energy = pressure * (1.0 / (GAMMA - 1.0)) + kinetic + magnetic
    return [density] + [density * v for v in vel] + [energy] + list(mag)


def step_kernel(
    count_o, count_i, blocks, reach,
    prim, moved,
    raw, tile, change, left, right, faces, x_before, x_after, y_send, y_before, y_after, ghost, edge,
    top_send, top_in, top_send2, top_in2,
    load_sem, x_sem, y_sem, in_sem, out_sem, low_sem, high_sem,
):
    tiles = raw.shape[0]
    total = count_o * count_i
    o, i = lax.axis_index("outer"), lax.axis_index("inner")
    me = o * count_i + i
    loads = [
        pltpu.make_async_copy(prim.at[:, pl.ds(t * LANES, LANES)], raw.at[t], load_sem.at[t])
        for t in range(tiles)
    ]
    for copy in loads:
        copy.start()

    def place_of(step):
        flat = lax.rem(me + (step % total), total)
        return (lax.div(flat, count_i), lax.rem(flat, count_i))

    def inner_id(k):
        return (o, lax.rem(i + 1 + k, count_i))

    def outer_id(k):
        return (lax.rem(o + 1 + k, count_o), i)

    barrier = pltpu.get_barrier_semaphore()

    def greet(target):
        pl.semaphore_signal(barrier, inc=1, device_id=target, device_id_type=MESH)

    @pl.loop(0, count_i - 1)
    def _(k):
        greet(inner_id(k))

    @pl.loop(0, count_o - 1)
    def _(k):
        greet(outer_id(k))

    for s in (1, -1, GY, -GY):
        greet(place_of(s))
    greeted = count_i + count_o + 2

    def send(src, dst, sems, index, target):
        return pltpu.make_async_remote_copy(
            src_ref=src, dst_ref=dst, send_sem=sems.at[0, index], recv_sem=sems.at[1, index],
            device_id=target, device_id_type=MESH,
        )

    lane = lax.broadcasted_iota(jnp.int32, (blocks, LANES), 1)
    quarter = lax.rem(lane, 64) // 16
    first_half = lane < 64
    even = lax.rem(lane, 16) < 8
    y_of = lax.rem(lane, 64) // 8
    z_of = lax.rem(lane, 8)
    y_first, y_last = y_of == 0, y_of == BE - 1
    z_first, z_last = z_of == 0, z_of == BE - 1

    for copy in loads:
        copy.wait()

    def gather(t, top):
        w = [raw[t, pl.ds(f, blocks, 8), :] for f in range(8)]
        for f in range(8):
            tile[t + 1, f] = w[f]
            a, b = turn(w[f], 16 * t), turn(w[f], lax.rem(16 * t + 80, LANES))
            mine = quarter == t
            y_send[0, f] = jnp.where(mine, a, y_send[0, f])
            y_send[1, f] = jnp.where(mine, b, y_send[1, f])
        field_sq = w[5] * w[5] + w[6] * w[6] + w[7] * w[7]
        signal = jnp.abs(w[1]) + jnp.abs(w[2]) + jnp.abs(w[3]) + 3.0 * sound(w[0], w[4], field_sq)
        return jnp.maximum(top, signal)

    top = lax.fori_loop(0, tiles, gather, jnp.zeros((blocks, LANES), jnp.float32))
    top_send[...] = jnp.max(top, axis=0, keepdims=True)
    pl.semaphore_wait(barrier, greeted)

    x_copies = [
        send(raw.at[tiles - 1], x_before, x_sem, 0, place_of(GY)),
        send(raw.at[0], x_after, x_sem, 1, place_of(-GY)),
    ]
    y_copies = [
        send(y_send.at[1], y_before, y_sem, 0, place_of(1)),
        send(y_send.at[0], y_after, y_sem, 1, place_of(-1)),
    ]
    for copy in y_copies:
        copy.start()

    def in_copy(k):
        return send(top_send, top_in.at[k], in_sem, k, inner_id(k))

    def out_copy(k):
        return send(top_send2, top_in2.at[k], out_sem, k, outer_id(k))

    @pl.loop(0, count_i - 1)
    def _(k):
        in_copy(k).start()

    for copy in x_copies:
        copy.start()

    def next_row(v):
        return jnp.concatenate([v[1:], v[:1]], axis=0)

    def prev_row(v):
        return jnp.concatenate([v[blocks - 1 :], v[: blocks - 1]], axis=0)

    @pl.loop(0, tiles)
    def _(t):
        lefts, rights = [], []
        for f in range(8):
            w = tile[t + 1, f]
            up = jnp.where(z_last, turn(next_row(w), 7), turn(w, -1))
            down = jnp.where(z_first, turn(prev_row(w), -7), turn(w, 1))
            h = half_slope(w - down, up - w)
            r = w - h
            lefts.append(w + h)
            rights.append(jnp.where(z_last, turn(next_row(r), 7), turn(r, -1)))
        g = face_flux(lefts, rights, 2)
        for f in range(8):
            before = jnp.where(z_first, turn(prev_row(g[f]), -7), turn(g[f], 1))
            change[t, f] = g[f] - before

    @pl.loop(0, count_i - 1)
    def _(k):
        in_copy(k).wait()

    row = top_send[...]
    for k in range(count_i - 1):
        row = jnp.maximum(row, top_in[k])
    top_send2[...] = row

    @pl.loop(0, count_o - 1)
    def _(k):
        out_copy(k).start()

    for copy in x_copies:
        copy.wait()
    for f in range(8):
        tile[0, f] = x_before[pl.ds(f, blocks, 8), :]
        tile[tiles + 1, f] = x_after[pl.ds(f, blocks, 8), :]

    def shift_x(low_tile, high_tile):
        return turn(jnp.where(first_half, low_tile, high_tile), 64)

    @pl.loop(0, tiles + 2)
    def _(t):
        over, under = jnp.minimum(t + 1, tiles + 1), jnp.maximum(t - 1, 0)
        for f in range(8):
            w = tile[t, f]
            up = shift_x(tile[over, f], w)
            down = shift_x(w, tile[under, f])
            h = half_slope(w - down, up - w)
            left[t, f] = w + h
            right[t, f] = w - h

    @pl.loop(0, tiles + 1)
    def _(t):
        g = face_flux(
            [left[t, f] for f in range(8)],
            [shift_x(right[t + 1, f], right[t, f]) for f in range(8)],
            0,
        )
        for f in range(8):
            faces[t, f] = g[f]

    for copy in y_copies:
        copy.wait()
    lefts, rights = [], []
    for f in range(8):
        low_own, high_own = y_send[0, f], y_send[1, f]
        before, after = y_before[f], y_after[f]
        a = jnp.where(even, high_own, turn(before, 72))
        b = jnp.where(even, turn(high_own, -8), turn(before, 64))
        c = jnp.where(even, after, turn(low_own, 72))
        d = jnp.where(even, turn(after, -8), turn(low_own, 64))
        mid = c - b
        lefts.append(b + half_slope(b - a, mid))
        rights.append(c - half_slope(mid, d - c))
        ghost[f] = jnp.where(even, c, b)
    g = face_flux(lefts, rights, 1)
    for f in range(8):
        edge[f] = g[f]

    @pl.loop(0, count_o - 1)
    def _(k):
        out_copy(k).wait()

    row = top_send2[...]
    for k in range(count_o - 1):
        row = jnp.maximum(row, top_in2[k])
    time_step = COURANT / jnp.max(row, axis=1, keepdims=True)

    low_rows = pl.ds(reach * 8, reach * 8)
    high_rows = pl.ds(blocks * 8, reach * 8)
    to_low_rows = pl.ds((reach + blocks) * 8, reach * 8)
    to_high_rows = pl.ds(0, reach * 8)

    def to_low(t):
        target = (o, lax.rem(i + count_i - 1, count_i))
        return send(moved.at[t, low_rows], moved.at[t, to_low_rows], low_sem, t, target)

    def to_high(t):
        target = (o, lax.rem(i + 1, count_i))
        return send(moved.at[t, high_rows], moved.at[t, to_high_rows], high_sem, t, target)

    @pl.loop(0, tiles)
    def _(t):
        back = lax.rem(56 + LANES - 16 * t, LANES)
        lefts, rights, w = [], [], []
        for f in range(8):
            w.append(tile[t + 1, f])
            rim = turn(ghost[f], back)
            up = jnp.where(y_last, rim, turn(w[f], -8))
            down = jnp.where(y_first, rim, turn(w[f], 8))
            h = half_slope(w[f] - down, up - w[f])
            lefts.append(w[f] + h)
            rights.append(turn(w[f] - h, -8))
        g = face_flux(lefts, rights, 1)
        cons = conserved(w)
        for f in range(8):
            rim = turn(edge[f], back)
            face = jnp.where(y_last, rim, g[f])
            before = jnp.where(y_first, rim, turn(g[f], 8))
            across = faces[t + 1, f]
            across = across - shift_x(across, faces[t, f])
            result = cons[f] - time_step * (across + (face - before) + change[t, f])
            moved[t, pl.ds(reach * 8 + f, blocks, 8), :] = result

        @pl.when(i > 0)
        def _():
            to_low(t).start()

        @pl.when(i < count_i - 1)
        def _():
            to_high(t).start()

    @pl.when(i > 0)
    def _():
        for t in range(tiles):
            to_low(t).wait_send()
            to_high(t).wait_recv()

    @pl.when(i < count_i - 1)
    def _():
        for t in range(tiles):
            to_high(t).wait_send()
            to_low(t).wait_recv()


def place_kernel(blocks, reach, block_total, count_i, owner, moved, out, wide, held, in_sem, out_sem):
    me = lax.axis_index("outer") * count_i + lax.axis_index("inner")
    capacity = blocks + 2 * reach
    fetch = pltpu.make_async_copy(moved, wide.at[:, pl.ds(0, capacity * 8)], in_sem)
    fetch.start()

    def look(c, carry):
        start, count = carry
        g = me * blocks - reach + c
        inside = (g >= 0) & (g < block_total)
        mine = inside & (owner[jnp.clip(g, 0, block_total - 1)] == me)
        return jnp.where(mine, jnp.minimum(start, c), start), count + mine.astype(jnp.int32)

    start, count = lax.fori_loop(0, capacity, look, (jnp.int32(2 * reach), jnp.int32(0)))
    live = lax.broadcasted_iota(jnp.int32, (capacity, LANES), 0) < count
    fetch.wait()

    def put(f):
        return pltpu.make_async_copy(held.at[f], out.at[f], out_sem.at[f])

    @pl.loop(0, 8)
    def _(f):
        for t in range(wide.shape[0]):
            held[f, :, t * LANES : (t + 1) * LANES] = jnp.where(
                live, wide[t, pl.ds(start * 8 + f, capacity, 8), :], 0.0
            )
        put(f).start()

    @pl.loop(0, 8)
    def _(f):
        put(f).wait()


def per_device(count_o, count_i, prim, new_owner, new_slot):
    blocks, cells = prim.shape[1:]
    reach = blocks // 2
    tiles = cells // LANES
    capacity = blocks + 2 * reach
    anywhere = pl.BlockSpec(memory_space=pl.ANY)
    vmem = pl.BlockSpec(memory_space=pltpu.VMEM)
    f32 = jnp.float32
    dma = pltpu.SemaphoreType.DMA

    def room(*lead):
        return pltpu.VMEM(lead + (8, blocks, LANES), f32)

    rows = prim.transpose(1, 0, 2).reshape(blocks * 8, cells)
    moved = pl.pallas_call(
        functools.partial(step_kernel, count_o, count_i, blocks, reach),
        out_shape=jax.ShapeDtypeStruct((tiles, capacity * 8, LANES), f32),
        in_specs=[anywhere],
        out_specs=vmem,
        scratch_shapes=[
            pltpu.VMEM((tiles, blocks * 8, LANES), f32),
            room(tiles + 2),
            room(tiles),
            room(tiles + 2),
            room(tiles + 2),
            room(tiles + 1),
            pltpu.VMEM((blocks * 8, LANES), f32),
            pltpu.VMEM((blocks * 8, LANES), f32),
            room(2),
            room(),
            room(),
            room(),
            room(),
            pltpu.VMEM((1, LANES), f32),
            pltpu.VMEM((count_i - 1, 1, LANES), f32),
            pltpu.VMEM((1, LANES), f32),
            pltpu.VMEM((count_o - 1, 1, LANES), f32),
            dma((tiles,)),
            dma((2, 2)),
            dma((2, 2)),
            dma((2, count_i - 1)),
            dma((2, count_o - 1)),
            dma((2, tiles)),
            dma((2, tiles)),
        ],
        compiler_params=pltpu.CompilerParams(collective_id=0, has_side_effects=True),
        name="step",
    )(rows)
    return pl.pallas_call(
        functools.partial(place_kernel, blocks, reach, new_owner.shape[0], count_i),
        out_shape=jax.ShapeDtypeStruct((8, capacity, cells), f32),
        in_specs=[pl.BlockSpec(memory_space=pltpu.SMEM), anywhere],
        out_specs=anywhere,
        scratch_shapes=[
            pltpu.VMEM((tiles, (capacity + 2 * reach) * 8, LANES), f32),
            pltpu.VMEM((8, capacity, cells), f32),
            dma,
            dma((8,)),
        ],
        name="place",
    )(new_owner, moved)


def solution(mesh):
    in_specs = (P(None, ("outer", "inner"), None), P(), P())
    out_specs = P(None, ("outer", "inner"), None)
    run = functools.partial(per_device, mesh.shape["outer"], mesh.shape["inner"])
    return jax.shard_map(
        run, mesh=mesh, in_specs=in_specs, out_specs=out_specs, check_vma=False
    )
```

time: 21.8 us -> 19.5 us (0.89)
  local copies, waits for them, and re-layouts: 1.75 us -> 0 us
  Pallas kernels: 19.9 us -> 19.3 us
    unnamed x1 -> x0, local copies, waits for them, and re-layouts: 1.75 us -> none
    pallas_call x1, Pallas kernels: 17.9 us -> 16.7 us  [per_device(): pl.pallas_call(functools.partial(step_kernel, count_o, count_i, blocks, r...]
    pallas_call x1, Pallas kernels: 2 us -> 2.52 us  [per_device(): pl.pallas_call(functools.partial(place_kernel, blocks, reach, new_owner.s...]
where the time goes in v2:
time: 19.5 us; the launch traced here: 19.3 us
  Pallas kernels  19.3 us (99%)
    pallas_call x1, Pallas kernels, per_device(): pl.pallas_call(functools.partial(step_kernel, count_o, count_i, blocks, r...  16.7 us
    pallas_call x1, Pallas kernels, per_device(): pl.pallas_call(functools.partial(place_kernel, blocks, reach, new_owner.s...  2.52 us

profile of v2, /device:TPU:1, one launch (start us, length us, event | category | flops | bytes accessed | tf_op | source)
XLA Modules:
  0.0 19.3 jit_solution(2150569410746851921)
XLA Ops:
  0.0 16.7 %step.1.moved = f32[4,192,128]{2,1,0:T(8,128)} custom-call(f32[96,512]{1,0:T(8,128)} %bitcast.3), custom_call_target="tpu_custom_call" | custom-call | tf_op jit(solution)/shard_map/step/pallas_call | solution.py:380
  16.8 2.5 %place.1 = f32[8,24,512]{2,1,0:T(8,128)} custom-call(s32[384]{0:T(512)} %owner.1, f32[4,192,128]{2,1,0:T(8,128)} %step.1.moved), custom_call_target="tpu_custom_call" | custom-call | tf_op jit(solution)/shard_map/place/pallas_call | solution.py:414

commit v3 on v2

--- a/solution.py
+++ b/solution.py
@@ -80,21 +80,25 @@
 
 def step_kernel(
     count_o, count_i, blocks, reach,
-    prim, moved,
-    raw, tile, change, left, right, faces, x_before, x_after, y_send, y_before, y_after, ghost, edge,
+    block_total, prim, owners, moved, state, fastest, run,
+    tile, change, left, right, faces, x_before, x_after, y_send, y_before, y_after, ghost, edge,
     top_send, top_in, top_send2, top_in2,
-    load_sem, x_sem, y_sem, in_sem, out_sem, low_sem, high_sem,
+    owner, load_sem, owner_sem, x_sem, y_sem, in_sem, out_sem, low_sem, high_sem, state_sem,
 ):
-    tiles = raw.shape[0]
+    tiles = state.shape[0]
+    capacity = blocks + 2 * reach
+    own_rows = pl.ds(reach * 8, blocks * 8)
     total = count_o * count_i
     o, i = lax.axis_index("outer"), lax.axis_index("inner")
     me = o * count_i + i
     loads = [
-        pltpu.make_async_copy(prim.at[:, pl.ds(t * LANES, LANES)], raw.at[t], load_sem.at[t])
+        pltpu.make_async_copy(prim.at[:, pl.ds(t * LANES, LANES)], state.at[t, own_rows], load_sem.at[t])
         for t in range(tiles)
     ]
     for copy in loads:
         copy.start()
+    owner_load = pltpu.make_async_copy(owners, owner, owner_sem)
+    owner_load.start()
 
     def place_of(step):
         flat = lax.rem(me + (step % total), total)
@@ -142,7 +146,7 @@
         copy.wait()
 
     def gather(t, top):
-        w = [raw[t, pl.ds(f, blocks, 8), :] for f in range(8)]
+        w = [state[t, pl.ds(reach * 8 + f, blocks, 8), :] for f in range(8)]
         for f in range(8):
             tile[t + 1, f] = w[f]
             a, b = turn(w[f], 16 * t), turn(w[f], lax.rem(16 * t + 80, LANES))
@@ -155,31 +159,6 @@
 
     top = lax.fori_loop(0, tiles, gather, jnp.zeros((blocks, LANES), jnp.float32))
     top_send[...] = jnp.max(top, axis=0, keepdims=True)
-    pl.semaphore_wait(barrier, greeted)
-
-    x_copies = [
-        send(raw.at[tiles - 1], x_before, x_sem, 0, place_of(GY)),
-        send(raw.at[0], x_after, x_sem, 1, place_of(-GY)),
-    ]
-    y_copies = [
-        send(y_send.at[1], y_before, y_sem, 0, place_of(1)),
-        send(y_send.at[0], y_after, y_sem, 1, place_of(-1)),
-    ]
-    for copy in y_copies:
-        copy.start()
-
-    def in_copy(k):
-        return send(top_send, top_in.at[k], in_sem, k, inner_id(k))
-
-    def out_copy(k):
-        return send(top_send2, top_in2.at[k], out_sem, k, outer_id(k))
-
-    @pl.loop(0, count_i - 1)
-    def _(k):
-        in_copy(k).start()
-
-    for copy in x_copies:
-        copy.start()
 
     def next_row(v):
         return jnp.concatenate([v[1:], v[:1]], axis=0)
@@ -202,6 +181,73 @@
         for f in range(8):
             before = jnp.where(z_first, turn(prev_row(g[f]), -7), turn(g[f], 1))
             change[t, f] = g[f] - before
+
+    pl.semaphore_wait(barrier, greeted)
+
+    x_copies = [
+        send(state.at[tiles - 1, own_rows], x_before, x_sem, 0, place_of(GY)),
+        send(state.at[0, own_rows], x_after, x_sem, 1, place_of(-GY)),
+    ]
+    y_copies = [
+        send(y_send.at[1], y_before, y_sem, 0, place_of(1)),
+        send(y_send.at[0], y_after, y_sem, 1, place_of(-1)),
+    ]
+    for copy in y_copies:
+        copy.start()
+
+    def in_copy(k):
+        return send(top_send, top_in.at[k], in_sem, k, inner_id(k))
+
+    def out_copy(k):
+        return send(top_send2, top_in2.at[k], out_sem, k, outer_id(k))
+
+    @pl.loop(0, count_i - 1)
+    def _(k):
+        in_copy(k).start()
+
+    for copy in x_copies:
+        copy.start()
+
+    low_rows = pl.ds(reach * 8, reach * 8)
+    high_rows = pl.ds(blocks * 8, reach * 8)
+    to_low_rows = pl.ds((reach + blocks) * 8, reach * 8)
+    to_high_rows = pl.ds(0, reach * 8)
+
+    def to_low(t):
+        target = (o, lax.rem(i + count_i - 1, count_i))
+        return send(moved.at[t, low_rows], moved.at[t, to_low_rows], low_sem, t, target)
+
+    def to_high(t):
+        target = (o, lax.rem(i + 1, count_i))
+        return send(moved.at[t, high_rows], moved.at[t, to_high_rows], high_sem, t, target)
+
+    state_low = send(
+        state.at[:, low_rows], state.at[:, to_low_rows], state_sem, 0, (o, lax.rem(i + count_i - 1, count_i))
+    )
+    state_high = send(
+        state.at[:, high_rows], state.at[:, to_high_rows], state_sem, 1, (o, lax.rem(i + 1, count_i))
+    )
+
+    @pl.when(i > 0)
+    def _():
+        state_low.start()
+
+    @pl.when(i < count_i - 1)
+    def _():
+        state_high.start()
+
+    owner_load.wait()
+
+    def look(c, carry):
+        start, count = carry
+        g = me * blocks - reach + c
+        inside = (g >= 0) & (g < block_total)
+        mine = inside & (owner[jnp.clip(g, 0, block_total - 1)] == me)
+        return jnp.where(mine, jnp.minimum(start, c), start), count + mine.astype(jnp.int32)
+
+    start, count = lax.fori_loop(0, capacity, look, (jnp.int32(2 * reach), jnp.int32(0)))
+    row_of = lax.broadcasted_iota(jnp.int32, run.shape, 0)
+    run[...] = jnp.where(row_of == 0, start, count)
 
     @pl.loop(0, count_i - 1)
     def _(k):
@@ -264,28 +310,6 @@
     for f in range(8):
         edge[f] = g[f]
 
-    @pl.loop(0, count_o - 1)
-    def _(k):
-        out_copy(k).wait()
-
-    row = top_send2[...]
-    for k in range(count_o - 1):
-        row = jnp.maximum(row, top_in2[k])
-    time_step = COURANT / jnp.max(row, axis=1, keepdims=True)
-
-    low_rows = pl.ds(reach * 8, reach * 8)
-    high_rows = pl.ds(blocks * 8, reach * 8)
-    to_low_rows = pl.ds((reach + blocks) * 8, reach * 8)
-    to_high_rows = pl.ds(0, reach * 8)
-
-    def to_low(t):
-        target = (o, lax.rem(i + count_i - 1, count_i))
-        return send(moved.at[t, low_rows], moved.at[t, to_low_rows], low_sem, t, target)
-
-    def to_high(t):
-        target = (o, lax.rem(i + 1, count_i))
-        return send(moved.at[t, high_rows], moved.at[t, to_high_rows], high_sem, t, target)
-
     @pl.loop(0, tiles)
     def _(t):
         back = lax.rem(56 + LANES - 16 * t, LANES)
@@ -299,14 +323,13 @@
             lefts.append(w[f] + h)
             rights.append(turn(w[f] - h, -8))
         g = face_flux(lefts, rights, 1)
-        cons = conserved(w)
         for f in range(8):
             rim = turn(edge[f], back)
             face = jnp.where(y_last, rim, g[f])
             before = jnp.where(y_first, rim, turn(g[f], 8))
             across = faces[t + 1, f]
             across = across - shift_x(across, faces[t, f])
-            result = cons[f] - time_step * (across + (face - before) + change[t, f])
+            result = across + (face - before) + change[t, f]
             moved[t, pl.ds(reach * 8 + f, blocks, 8), :] = result
 
         @pl.when(i > 0)
@@ -316,51 +339,55 @@
         @pl.when(i < count_i - 1)
         def _():
             to_high(t).start()
+
+    @pl.loop(0, count_o - 1)
+    def _(k):
+        out_copy(k).wait()
+
+    row = top_send2[...]
+    for k in range(count_o - 1):
+        row = jnp.maximum(row, top_in2[k])
+    fastest[...] = row
 
     @pl.when(i > 0)
     def _():
         for t in range(tiles):
             to_low(t).wait_send()
             to_high(t).wait_recv()
+        state_low.wait_send()
+        state_high.wait_recv()
 
     @pl.when(i < count_i - 1)
     def _():
         for t in range(tiles):
             to_high(t).wait_send()
             to_low(t).wait_recv()
-
-
-def place_kernel(blocks, reach, block_total, count_i, owner, moved, out, wide, held, in_sem, out_sem):
-    me = lax.axis_index("outer") * count_i + lax.axis_index("inner")
-    capacity = blocks + 2 * reach
-    fetch = pltpu.make_async_copy(moved, wide.at[:, pl.ds(0, capacity * 8)], in_sem)
-    fetch.start()
-
-    def look(c, carry):
-        start, count = carry
-        g = me * blocks - reach + c
-        inside = (g >= 0) & (g < block_total)
-        mine = inside & (owner[jnp.clip(g, 0, block_total - 1)] == me)
-        return jnp.where(mine, jnp.minimum(start, c), start), count + mine.astype(jnp.int32)
-
-    start, count = lax.fori_loop(0, capacity, look, (jnp.int32(2 * reach), jnp.int32(0)))
+        state_high.wait_send()
+        state_low.wait_recv()
+
+
+def place_kernel(capacity, moved, state, fastest, run, out, held, out_sem):
+    tiles = state.shape[0]
+    start = jnp.max(run[pl.ds(0, 1), :])
+    count = jnp.max(run[pl.ds(1, 1), :])
     live = lax.broadcasted_iota(jnp.int32, (capacity, LANES), 0) < count
-    fetch.wait()
-
-    def put(f):
-        return pltpu.make_async_copy(held.at[f], out.at[f], out_sem.at[f])
-
-    @pl.loop(0, 8)
-    def _(f):
-        for t in range(wide.shape[0]):
-            held[f, :, t * LANES : (t + 1) * LANES] = jnp.where(
-                live, wide[t, pl.ds(start * 8 + f, capacity, 8), :], 0.0
-            )
-        put(f).start()
-
-    @pl.loop(0, 8)
-    def _(f):
-        put(f).wait()
+    time_step = COURANT / jnp.max(fastest[...], axis=1, keepdims=True)
+
+    def put(t):
+        spot = pl.ds(pl.multiple_of(t * LANES, LANES), LANES)
+        return pltpu.make_async_copy(held.at[t], out.at[:, :, spot], out_sem.at[t])
+
+    @pl.loop(0, tiles)
+    def _(t):
+        rows = [pl.ds(start * 8 + f, capacity, 8) for f in range(8)]
+        cons = conserved([state[t, rows[f], :] for f in range(8)])
+        for f in range(8):
+            held[t, f] = jnp.where(live, cons[f] - time_step * moved[t, rows[f], :], 0.0)
+        put(t).start()
+
+    @pl.loop(0, tiles)
+    def _(t):
+        put(t).wait()
 
 
 def per_device(count_o, count_i, prim, new_owner, new_slot):
@@ -377,13 +404,17 @@
         return pltpu.VMEM(lead + (8, blocks, LANES), f32)
 
     rows = prim.transpose(1, 0, 2).reshape(blocks * 8, cells)
-    moved = pl.pallas_call(
-        functools.partial(step_kernel, count_o, count_i, blocks, reach),
-        out_shape=jax.ShapeDtypeStruct((tiles, capacity * 8, LANES), f32),
-        in_specs=[anywhere],
-        out_specs=vmem,
+    handed = pl.pallas_call(
+        functools.partial(step_kernel, count_o, count_i, blocks, reach, new_owner.shape[0]),
+        out_shape=[
+            pltpu.VMEM((tiles, (capacity + 2 * reach) * 8, LANES), f32),
+            pltpu.VMEM((tiles, (capacity + 2 * reach) * 8, LANES), f32),
+            pltpu.VMEM((1, LANES), f32),
+            pltpu.VMEM((2, LANES), jnp.int32),
+        ],
+        in_specs=[anywhere, anywhere],
+        out_specs=[vmem] * 4,
         scratch_shapes=[
-            pltpu.VMEM((tiles, blocks * 8, LANES), f32),
             room(tiles + 2),
             room(tiles),
             room(tiles + 2),
@@ -400,30 +431,28 @@
             pltpu.VMEM((count_i - 1, 1, LANES), f32),
             pltpu.VMEM((1, LANES), f32),
             pltpu.VMEM((count_o - 1, 1, LANES), f32),
+            pltpu.SMEM(new_owner.shape, jnp.int32),
             dma((tiles,)),
+            dma,
             dma((2, 2)),
             dma((2, 2)),
             dma((2, count_i - 1)),
             dma((2, count_o - 1)),
             dma((2, tiles)),
             dma((2, tiles)),
+            dma((2, 2)),
         ],
         compiler_params=pltpu.CompilerParams(collective_id=0, has_side_effects=True),
         name="step",
-    )(rows)
+    )(rows, new_owner)
     return pl.pallas_call(
-        functools.partial(place_kernel, blocks, reach, new_owner.shape[0], count_i),
+        functools.partial(place_kernel, capacity),
         out_shape=jax.ShapeDtypeStruct((8, capacity, cells), f32),
-        in_specs=[pl.BlockSpec(memory_space=pltpu.SMEM), anywhere],
+        in_specs=[vmem] * 4,
         out_specs=anywhere,
-        scratch_shapes=[
-            pltpu.VMEM((tiles, (capacity + 2 * reach) * 8, LANES), f32),
-            pltpu.VMEM((8, capacity, cells), f32),
-            dma,
-            dma((8,)),
-        ],
+        scratch_shapes=[pltpu.VMEM((tiles, 8, capacity, LANES), f32), dma((tiles,))],
         name="place",
-    )(new_owner, moved)
+    )(*[pltpu.with_memory_space_constraint(part, pltpu.VMEM) for part in handed])
 
 
 def solution(mesh):

time: 19.5 us -> 16.1 us (0.83)
  Pallas kernels: 19.3 us -> 15.9 us
    pallas_call x1, Pallas kernels: 16.7 us -> 14.8 us  [per_device(): pl.pallas_call(functools.partial(step_kernel, count_o, count_i, blocks, r...]
    pallas_call x1, Pallas kernels: 2.52 us -> 1.04 us  [per_device(): pl.pallas_call(functools.partial(place_kernel, capacity), out_shape=jax.S...]
where the time goes in v3:
time: 16.1 us; the launch traced here: 15.9 us
  Pallas kernels  15.9 us (99%)
    pallas_call x1, Pallas kernels, per_device(): pl.pallas_call(functools.partial(step_kernel, count_o, count_i, blocks, r...  14.8 us
    pallas_call x1, Pallas kernels, per_device(): pl.pallas_call(functools.partial(place_kernel, capacity), out_shape=jax.S...  1.04 us

profile of v3, /device:TPU:1, one launch (start us, length us, event | category | flops | bytes accessed | tf_op | source)
XLA Modules:
  0.0 15.9 jit_solution(264855274598348123)
XLA Ops:
  0.0 14.8 %step.1 = (f32[4,288,128]{2,1,0:T(8,128)S(1)}, f32[4,288,128]{2,1,0:T(8,128)S(1)}, f32[1,128]{1,0:T(1,128)S(1)}, s32[2,128]{1,0:T(2,128)S(1)}) custom-call(f32[96,512]{1,0:T(8,128)} %bitcast.3, s32[384]{0:T(512)} %owners.1), custom_call_target="tpu_custom_call" | custom-call | tf_op jit(solution)/shard_map/step/pallas_call | solution.py:407
  14.8 1.0 %place.1 = f32[8,24,512]{2,1,0:T(8,128)} custom-call(f32[4,288,128]{2,1,0:T(8,128)S(1)} %get-tuple-element.9.moved, f32[4,288,128]{2,1,0:T(8,128)S(1)} %get-tuple-element.10.state, f32[1,128]{1,0:T(1,128)S(1)} %get-tuple-element.11.fastest, s32[2,128]{1,0:T(2,128)S(1)} %get-tuple-element.12.run), custom_call_target="tpu_custom_call" | custom-call | tf_op jit(solution)/shard_map/place/pallas_call | solution.py:448

commit v4 on v3

--- a/solution.py
+++ b/solution.py
@@ -81,7 +81,7 @@
 def step_kernel(
     count_o, count_i, blocks, reach,
     block_total, prim, owners, moved, state, fastest, run,
-    tile, change, left, right, faces, x_before, x_after, y_send, y_before, y_after, ghost, edge,
+    tile, change, left, right, faces, x_before, x_after, y_send, y_before, y_after, inner, edge, near,
     top_send, top_in, top_send2, top_in2,
     owner, load_sem, owner_sem, x_sem, y_sem, in_sem, out_sem, low_sem, high_sem, state_sem,
 ):
@@ -139,7 +139,10 @@
     even = lax.rem(lane, 16) < 8
     y_of = lax.rem(lane, 64) // 8
     z_of = lax.rem(lane, 8)
-    y_first, y_last = y_of == 0, y_of == BE - 1
+    y_inside = (y_of >= 1) & (y_of <= BE - 3)
+    y_rim = (y_of == 0) | (y_of == BE - 1)
+    y_near = (y_of == 1) | (y_of == BE - 2)
+    packed_tile = jnp.where(even, quarter, lax.rem(lane + 40, 64) // 16)
     z_first, z_last = z_of == 0, z_of == BE - 1
 
     for copy in loads:
@@ -181,6 +184,22 @@
         for f in range(8):
             before = jnp.where(z_first, turn(prev_row(g[f]), -7), turn(g[f], 1))
             change[t, f] = g[f] - before
+
+    @pl.loop(0, tiles)
+    def _(t):
+        ahead = lax.rem(80 + 16 * t, LANES)
+        lefts, rights = [], []
+        for f in range(8):
+            w = tile[t + 1, f]
+            h = half_slope(w - turn(w, 8), turn(w, -8) - w)
+            lefts.append(w + h)
+            rights.append(turn(w - h, -8))
+            beside = turn(jnp.where(y_of == 1, w - h, w + h), ahead)
+            inner[f] = jnp.where(packed_tile == t, beside, inner[f])
+        g = face_flux(lefts, rights, 1)
+        for f in range(8):
+            kept = jnp.where(y_inside, g[f], 0.0)
+            change[t, f] = change[t, f] + (kept - turn(kept, 8))
 
     pl.semaphore_wait(barrier, greeted)
 
@@ -262,17 +281,25 @@
     def _(k):
         out_copy(k).start()
 
-    for copy in x_copies:
-        copy.wait()
-    for f in range(8):
-        tile[0, f] = x_before[pl.ds(f, blocks, 8), :]
-        tile[tiles + 1, f] = x_after[pl.ds(f, blocks, 8), :]
-
     def shift_x(low_tile, high_tile):
         return turn(jnp.where(first_half, low_tile, high_tile), 64)
 
     @pl.loop(0, tiles + 2)
-    def _(t):
+    def _(k):
+        @pl.when(k == tiles - 2)
+        def _():
+            x_copies[0].wait()
+            for f in range(8):
+                tile[0, f] = x_before[pl.ds(f, blocks, 8), :]
+
+        @pl.when(k == tiles)
+        def _():
+            x_copies[1].wait()
+            for f in range(8):
+                tile[tiles + 1, f] = x_after[pl.ds(f, blocks, 8), :]
+
+        t = jnp.where(k < tiles, tiles - 1 - k, k)
+        face = jnp.where(k < tiles, t, t - 1)
         over, under = jnp.minimum(t + 1, tiles + 1), jnp.maximum(t - 1, 0)
         for f in range(8):
             w = tile[t, f]
@@ -281,20 +308,17 @@
             h = half_slope(w - down, up - w)
             left[t, f] = w + h
             right[t, f] = w - h
-
-    @pl.loop(0, tiles + 1)
-    def _(t):
         g = face_flux(
-            [left[t, f] for f in range(8)],
-            [shift_x(right[t + 1, f], right[t, f]) for f in range(8)],
+            [left[face, f] for f in range(8)],
+            [shift_x(right[face + 1, f], right[face, f]) for f in range(8)],
             0,
         )
         for f in range(8):
-            faces[t, f] = g[f]
+            faces[face, f] = g[f]
 
     for copy in y_copies:
         copy.wait()
-    lefts, rights = [], []
+    lefts, rights, inner_lefts, inner_rights = [], [], [], []
     for f in range(8):
         low_own, high_own = y_send[0, f], y_send[1, f]
         before, after = y_before[f], y_after[f]
@@ -303,33 +327,31 @@
         c = jnp.where(even, after, turn(low_own, 72))
         d = jnp.where(even, turn(after, -8), turn(low_own, 64))
         mid = c - b
-        lefts.append(b + half_slope(b - a, mid))
-        rights.append(c - half_slope(mid, d - c))
-        ghost[f] = jnp.where(even, c, b)
+        h_b, h_c = half_slope(b - a, mid), half_slope(mid, d - c)
+        lefts.append(b + h_b)
+        rights.append(c - h_c)
+        p = inner[f]
+        p = jnp.where(even, p, turn(p, -16))
+        inner_lefts.append(jnp.where(even, p, c + h_c))
+        inner_rights.append(jnp.where(even, b - h_b, p))
     g = face_flux(lefts, rights, 1)
+    g_inner = face_flux(inner_lefts, inner_rights, 1)
     for f in range(8):
-        edge[f] = g[f]
+        between = g[f] - g_inner[f]
+        edge[f] = jnp.where(even, between, -between)
+        near[f] = jnp.where(even, g_inner[f], -turn(g_inner[f], 16))
 
     @pl.loop(0, tiles)
     def _(t):
-        back = lax.rem(56 + LANES - 16 * t, LANES)
-        lefts, rights, w = [], [], []
-        for f in range(8):
-            w.append(tile[t + 1, f])
-            rim = turn(ghost[f], back)
-            up = jnp.where(y_last, rim, turn(w[f], -8))
-            down = jnp.where(y_first, rim, turn(w[f], 8))
-            h = half_slope(w[f] - down, up - w[f])
-            lefts.append(w[f] + h)
-            rights.append(turn(w[f] - h, -8))
-        g = face_flux(lefts, rights, 1)
-        for f in range(8):
-            rim = turn(edge[f], back)
-            face = jnp.where(y_last, rim, g[f])
-            before = jnp.where(y_first, rim, turn(g[f], 8))
+        rim_back = lax.rem(56 + LANES - 16 * t, LANES)
+        near_back = lax.rem(48 + LANES - 16 * t, LANES)
+        for f in range(8):
             across = faces[t + 1, f]
             across = across - shift_x(across, faces[t, f])
-            result = across + (face - before) + change[t, f]
+            added = jnp.where(
+                y_rim, turn(edge[f], rim_back), jnp.where(y_near, turn(near[f], near_back), 0.0)
+            )
+            result = across + (change[t, f] + added)
             moved[t, pl.ds(reach * 8 + f, blocks, 8), :] = result
 
         @pl.when(i > 0)
@@ -423,6 +445,7 @@
             pltpu.VMEM((blocks * 8, LANES), f32),
             pltpu.VMEM((blocks * 8, LANES), f32),
             room(2),
+            room(),
             room(),
             room(),
             room(),

time: 16.1 us -> 17 us (1.056)
  Pallas kernels: 15.9 us -> 16.8 us
    pallas_call x1, Pallas kernels: 14.8 us -> 15.8 us  [per_device(): pl.pallas_call(functools.partial(step_kernel, count_o, count_i, blocks, r...]
where the time goes in v4:
time: 17 us; the launch traced here: 16.9 us
  Pallas kernels  16.8 us (99%)
    pallas_call x1, Pallas kernels, per_device(): pl.pallas_call(functools.partial(step_kernel, count_o, count_i, blocks, r...  15.8 us
    pallas_call x1, Pallas kernels, per_device(): pl.pallas_call(functools.partial(place_kernel, capacity), out_shape=jax.S...  1.04 us

profile of v4, /device:TPU:1, one launch (start us, length us, event | category | flops | bytes accessed | tf_op | source)
XLA Modules:
  0.0 16.9 jit_solution(4050055138820129390)
XLA Ops:
  0.0 15.8 %step.1 = (f32[4,288,128]{2,1,0:T(8,128)S(1)}, f32[4,288,128]{2,1,0:T(8,128)S(1)}, f32[1,128]{1,0:T(1,128)S(1)}, s32[2,128]{1,0:T(2,128)S(1)}) custom-call(f32[96,512]{1,0:T(8,128)} %bitcast.3, s32[384]{0:T(512)} %owners.1), custom_call_target="tpu_custom_call" | custom-call | tf_op jit(solution)/shard_map/step/pallas_call | solution.py:429
  15.8 1.0 %place.1 = f32[8,24,512]{2,1,0:T(8,128)} custom-call(f32[4,288,128]{2,1,0:T(8,128)S(1)} %get-tuple-element.9.moved, f32[4,288,128]{2,1,0:T(8,128)S(1)} %get-tuple-element.10.state, f32[1,128]{1,0:T(1,128)S(1)} %get-tuple-element.11.fastest, s32[2,128]{1,0:T(2,128)S(1)} %get-tuple-element.12.run), custom_call_target="tpu_custom_call" | custom-call | tf_op jit(solution)/shard_map/place/pallas_call | solution.py:471

commit v5 on v4

--- a/solution.py
+++ b/solution.py
@@ -163,44 +163,6 @@
     top = lax.fori_loop(0, tiles, gather, jnp.zeros((blocks, LANES), jnp.float32))
     top_send[...] = jnp.max(top, axis=0, keepdims=True)
 
-    def next_row(v):
-        return jnp.concatenate([v[1:], v[:1]], axis=0)
-
-    def prev_row(v):
-        return jnp.concatenate([v[blocks - 1 :], v[: blocks - 1]], axis=0)
-
-    @pl.loop(0, tiles)
-    def _(t):
-        lefts, rights = [], []
-        for f in range(8):
-            w = tile[t + 1, f]
-            up = jnp.where(z_last, turn(next_row(w), 7), turn(w, -1))
-            down = jnp.where(z_first, turn(prev_row(w), -7), turn(w, 1))
-            h = half_slope(w - down, up - w)
-            r = w - h
-            lefts.append(w + h)
-            rights.append(jnp.where(z_last, turn(next_row(r), 7), turn(r, -1)))
-        g = face_flux(lefts, rights, 2)
-        for f in range(8):
-            before = jnp.where(z_first, turn(prev_row(g[f]), -7), turn(g[f], 1))
-            change[t, f] = g[f] - before
-
-    @pl.loop(0, tiles)
-    def _(t):
-        ahead = lax.rem(80 + 16 * t, LANES)
-        lefts, rights = [], []
-        for f in range(8):
-            w = tile[t + 1, f]
-            h = half_slope(w - turn(w, 8), turn(w, -8) - w)
-            lefts.append(w + h)
-            rights.append(turn(w - h, -8))
-            beside = turn(jnp.where(y_of == 1, w - h, w + h), ahead)
-            inner[f] = jnp.where(packed_tile == t, beside, inner[f])
-        g = face_flux(lefts, rights, 1)
-        for f in range(8):
-            kept = jnp.where(y_inside, g[f], 0.0)
-            change[t, f] = change[t, f] + (kept - turn(kept, 8))
-
     pl.semaphore_wait(barrier, greeted)
 
     x_copies = [
@@ -267,6 +229,44 @@
     start, count = lax.fori_loop(0, capacity, look, (jnp.int32(2 * reach), jnp.int32(0)))
     row_of = lax.broadcasted_iota(jnp.int32, run.shape, 0)
     run[...] = jnp.where(row_of == 0, start, count)
+
+    def next_row(v):
+        return jnp.concatenate([v[1:], v[:1]], axis=0)
+
+    def prev_row(v):
+        return jnp.concatenate([v[blocks - 1 :], v[: blocks - 1]], axis=0)
+
+    @pl.loop(0, tiles)
+    def _(t):
+        lefts, rights = [], []
+        for f in range(8):
+            w = tile[t + 1, f]
+            up = jnp.where(z_last, turn(next_row(w), 7), turn(w, -1))
+            down = jnp.where(z_first, turn(prev_row(w), -7), turn(w, 1))
+            h = half_slope(w - down, up - w)
+            r = w - h
+            lefts.append(w + h)
+            rights.append(jnp.where(z_last, turn(next_row(r), 7), turn(r, -1)))
+        g = face_flux(lefts, rights, 2)
+        for f in range(8):
+            before = jnp.where(z_first, turn(prev_row(g[f]), -7), turn(g[f], 1))
+            change[t, f] = g[f] - before
+
+    @pl.loop(0, tiles)
+    def _(t):
+        ahead = lax.rem(80 + 16 * t, LANES)
+        lefts, rights = [], []
+        for f in range(8):
+            w = tile[t + 1, f]
+            h = half_slope(w - turn(w, 8), turn(w, -8) - w)
+            lefts.append(w + h)
+            rights.append(turn(w - h, -8))
+            beside = turn(jnp.where(y_of == 1, w - h, w + h), ahead)
+            inner[f] = jnp.where(packed_tile == t, beside, inner[f])
+        g = face_flux(lefts, rights, 1)
+        for f in range(8):
+            kept = jnp.where(y_inside, g[f], 0.0)
+            change[t, f] = change[t, f] + (kept - turn(kept, 8))
 
     @pl.loop(0, count_i - 1)
     def _(k):

time: 17 us -> 16.1 us (0.947)
  Pallas kernels: 16.8 us -> 15.9 us
    pallas_call x1, Pallas kernels: 15.8 us -> 14.9 us  [per_device(): pl.pallas_call(functools.partial(step_kernel, count_o, count_i, blocks, r...]
where the time goes in v5:
time: 16.1 us; the launch traced here: 16 us
  Pallas kernels  15.9 us (99%)
    pallas_call x1, Pallas kernels, per_device(): pl.pallas_call(functools.partial(step_kernel, count_o, count_i, blocks, r...  14.9 us
    pallas_call x1, Pallas kernels, per_device(): pl.pallas_call(functools.partial(place_kernel, capacity), out_shape=jax.S...  1.04 us

profile of v5, /device:TPU:1, one launch (start us, length us, event | category | flops | bytes accessed | tf_op | source)
XLA Modules:
  0.0 16.0 jit_solution(1550005067377574917)
XLA Ops:
  0.0 14.9 %step.1 = (f32[4,288,128]{2,1,0:T(8,128)S(1)}, f32[4,288,128]{2,1,0:T(8,128)S(1)}, f32[1,128]{1,0:T(1,128)S(1)}, s32[2,128]{1,0:T(2,128)S(1)}) custom-call(f32[96,512]{1,0:T(8,128)} %bitcast.3, s32[384]{0:T(512)} %owners.1), custom_call_target="tpu_custom_call" | custom-call | tf_op jit(solution)/shard_map/step/pallas_call | solution.py:429
  14.9 1.0 %place.1 = f32[8,24,512]{2,1,0:T(8,128)} custom-call(f32[4,288,128]{2,1,0:T(8,128)S(1)} %get-tuple-element.9.moved, f32[4,288,128]{2,1,0:T(8,128)S(1)} %get-tuple-element.10.state, f32[1,128]{1,0:T(1,128)S(1)} %get-tuple-element.11.fastest, s32[2,128]{1,0:T(2,128)S(1)} %get-tuple-element.12.run), custom_call_target="tpu_custom_call" | custom-call | tf_op jit(solution)/shard_map/place/pallas_call | solution.py:471
